TPU v7x, 32 devices: a whole 2x2x4 slice. The times are simulated.
32 devices in a mesh: slab: 8 (over z, x), pencil: 4 (over y, core).
Axes of the slice: x: 2, y: 2, z: 4, core: 2. Of those that a mesh axis runs over, the one named last changes fastest.
Arguments:
- sample_tile: int32 [8192, 1], P(('slab', 'pencil')), may hold values from 0 to 31; in each aligned block of 256 rows (0 to 255, 256 to 511, ...) at most 16 rows name the same one
- sample_cell: int32 [3, 8192], P(None, ('slab', 'pencil')), may hold values from 0 to 511, as said below
- sample_frac: float32 [3, 8192], P(None, ('slab', 'pencil')), may hold values from 0 to 1
- sample_value: float32 [2, 8192], P(None, ('slab', 'pencil')), may hold values from -24 to 24
Outputs:
- volume: float32 [2, 64, 512, 512], P(None, None, 'slab', 'pencil')
Inputs may be any that keep to these rules, and one draw needn't show every extreme that they name: `sample_tile`: among the 256 samples of one device no tile is named more than 16 times, and that count is reached in some device's block. `sample_cell`: row 0 is below 8, row 1 below 128, row 2 below 512.
All inputs are finite; a program needn't handle non-finite values.
Results may differ from a plain program's by a relative error of at most 0.0003.
Values sent between devices are 32-bit elements; how exact they have to be, the bound alone decides.
No kernel may reach another device: no remote copies, remote signals or barrier semaphores. Data moves between devices by JAX's collectives and lax.ppermute only.
A program may use at most 64 MiB of HBM per device.

v0:
```python
import math

import jax
import jax.numpy as jnp
from jax import lax
from jax.sharding import PartitionSpec as P

NY = 512
NX = 512
PLANES = 8


beta_shape = 18.64


def from_behind(block, axis, distance):
    devices = range(lax.axis_size(axis))
    route = [((i - distance) % len(devices), i) for i in devices]
    return lax.ppermute(block, axis, route)


def bessel_zero(value):
    quarter = value * value * 0.25
    term = jnp.ones_like(value)
    total = jnp.ones_like(value)
    for order in range(1, 41):
        term = term * quarter / float(order * order)
        total = total + term
    return total


def kernel_weights(offset):
    tap_offsets = jnp.arange(8, dtype=jnp.float32) - 3.0
    scaled_gap = (tap_offsets[None, :] - offset[:, None]) * 0.25
    radicand = jnp.maximum(1.0 - scaled_gap * scaled_gap, 0.0)
    numerator = bessel_zero(beta_shape * jnp.sqrt(radicand))
    return numerator / bessel_zero(jnp.full((), beta_shape, jnp.float32))


def dft_tables(length):
    counter = jnp.arange(length, dtype=jnp.int32)
    phase_index = counter[:, None] * counter[None, :] % length
    angles = phase_index.astype(jnp.float32) * jnp.float32(2.0 * math.pi / length)
    factor = jnp.float32(1.0 / math.sqrt(length))
    cosine = jnp.cos(angles) * factor
    sine = jnp.sin(angles) * factor
    return (cosine, sine, cosine + sine)


def placed_weights(tap_weight, anchor, length, wrap):
    positions = jnp.arange(length, dtype=jnp.int32)
    placed = jnp.zeros((anchor.shape[0], length), jnp.float32)
    for tap in range(8):
        where_at = anchor + tap
        if wrap:
            where_at = where_at % length
        hit = (positions[None, :] == where_at[:, None]).astype(jnp.float32)
        placed = placed + hit * tap_weight[:, tap][:, None]
    return placed


def spread_grid(cells, records, depth_cells, row_count):
    sample_count = cells.shape[1]
    height_cells = row_count + 7
    weight_z = kernel_weights(records[0])
    weight_y = kernel_weights(records[1])
    weight_x = kernel_weights(records[2])
    plane_table = placed_weights(weight_z, cells[0], depth_cells, False)
    row_table = placed_weights(weight_y, cells[1], height_cells, False)
    column_table = placed_weights(weight_x, cells[2], NX, True)
    left_table = (plane_table[:, :, None] * row_table[:, None, :]).reshape(
        sample_count, depth_cells * height_cells
    )
    real_right = column_table * records[3][:, None]
    imag_right = column_table * records[4][:, None]
    numbers = (((0,), (0,)), ((), ()))
    real_grid = lax.dot_general(
        left_table,
        real_right,
        numbers,
        precision=lax.Precision.HIGHEST,
        preferred_element_type=jnp.float32,
    )
    imag_grid = lax.dot_general(
        left_table,
        imag_right,
        numbers,
        precision=lax.Precision.HIGHEST,
        preferred_element_type=jnp.float32,
    )
    return jnp.stack([real_grid, imag_grid]).reshape(2, depth_cells, height_cells, NX)


def product(left, right):
    return jnp.dot(left, right, precision=lax.Precision.HIGHEST, preferred_element_type=jnp.float32)


def shards(sample_tile, sample_cell, sample_frac, sample_value):
    n_slab = lax.axis_size("slab")
    n_pencil = lax.axis_size("pencil")
    tile_count = n_slab * n_pencil
    sample_count = sample_tile.shape[0]
    capacity = max(2, 2 * sample_count // tile_count)
    row_count = NY // n_pencil
    planes = PLANES
    owner_tile = sample_tile[:, 0]
    sort_order = jnp.argsort(owner_tile, stable=True)
    sorted_owner = owner_tile[sort_order]
    tile_ids = jnp.arange(tile_count, dtype=jnp.int32)
    tile_loads = jnp.sum((sorted_owner[:, None] == tile_ids[None, :]).astype(jnp.int32), axis=0)
    starts = jnp.cumsum(tile_loads) - tile_loads
    sorted_rank = jnp.arange(sample_count, dtype=jnp.int32) - starts[sorted_owner]
    slot_rank = jnp.zeros((sample_count,), jnp.int32).at[sort_order].set(sorted_rank)
    records = jnp.concatenate([sample_frac, sample_value], axis=0)
    slot_count = 2 * capacity
    next_owner = (owner_tile // n_pencil + 1) % n_slab * n_pencil + owner_tile % n_pencil
    lowered = sample_cell.at[0].add(-planes)
    first_slot = owner_tile * slot_count + slot_rank
    second_slot = next_owner * slot_count + capacity + slot_rank
    cell_buffer = jnp.zeros((3, tile_count * slot_count), jnp.int32)
    cell_buffer = cell_buffer.at[:, first_slot].set(sample_cell).at[:, second_slot].set(lowered)
    record_buffer = jnp.zeros((5, tile_count * slot_count), jnp.float32)
    record_buffer = record_buffer.at[:, first_slot].set(records).at[:, second_slot].set(records)
    cell_buffer = cell_buffer.reshape(3, n_slab, n_pencil, slot_count)
    record_buffer = record_buffer.reshape(5, n_slab, n_pencil, slot_count)
    got_cells, got_records = (
        lax.all_to_all(
            lax.all_to_all(cell_buffer, "slab", split_axis=1, concat_axis=1, tiled=True),
            "pencil",
            split_axis=2,
            concat_axis=2,
            tiled=True,
        ),
        lax.all_to_all(
            lax.all_to_all(record_buffer, "slab", split_axis=1, concat_axis=1, tiled=True),
            "pencil",
            split_axis=2,
            concat_axis=2,
            tiled=True,
        ),
    )
    field_grid = spread_grid(
        got_cells.reshape(3, -1), got_records.reshape(5, -1), planes, row_count
    )
    row_rim = from_behind(field_grid[:, :, row_count:], "pencil", 1)
    field_grid = field_grid[:, :, :row_count].at[:, :, :7].add(row_rim)
    cos_x, sin_x, both_x = dft_tables(NX)
    flat_real = field_grid[0].reshape(planes * row_count, NX)
    flat_imag = field_grid[1].reshape(planes * row_count, NX)
    first_term = product(flat_real, cos_x)
    second_term = product(flat_imag, sin_x)
    third_term = product(flat_real + flat_imag, both_x)
    turned_real = (first_term - second_term).reshape(planes, row_count, NX)
    turned_imag = (third_term - first_term - second_term).reshape(planes, row_count, NX)
    cos_y, sin_y, both_y = dft_tables(NY)
    part_real = lax.all_to_all(turned_real, "pencil", split_axis=2, concat_axis=1, tiled=True)
    part_imag = lax.all_to_all(turned_imag, "pencil", split_axis=2, concat_axis=1, tiled=True)
    first_part = jnp.einsum(
        "nyx,ym->nmx",
        part_real,
        cos_y,
        precision=lax.Precision.HIGHEST,
        preferred_element_type=jnp.float32,
    )
    second_part = jnp.einsum(
        "nyx,ym->nmx",
        part_imag,
        sin_y,
        precision=lax.Precision.HIGHEST,
        preferred_element_type=jnp.float32,
    )
    third_part = jnp.einsum(
        "nyx,ym->nmx",
        part_real + part_imag,
        both_y,
        precision=lax.Precision.HIGHEST,
        preferred_element_type=jnp.float32,
    )
    middle_real = first_part - second_part
    middle_imag = third_part - first_part - second_part
    cos_z, sin_z, both_z = dft_tables(planes * n_slab)
    part_real = lax.all_to_all(middle_real, "slab", split_axis=1, concat_axis=0, tiled=True)
    part_imag = lax.all_to_all(middle_imag, "slab", split_axis=1, concat_axis=0, tiled=True)
    first_part = jnp.einsum(
        "zyx,zm->myx",
        part_real,
        cos_z,
        precision=lax.Precision.HIGHEST,
        preferred_element_type=jnp.float32,
    )
    second_part = jnp.einsum(
        "zyx,zm->myx",
        part_imag,
        sin_z,
        precision=lax.Precision.HIGHEST,
        preferred_element_type=jnp.float32,
    )
    third_part = jnp.einsum(
        "zyx,zm->myx",
        part_real + part_imag,
        both_z,
        precision=lax.Precision.HIGHEST,
        preferred_element_type=jnp.float32,
    )
    final_real = first_part - second_part
    final_imag = third_part - first_part - second_part
    return jnp.stack([final_real, final_imag])


def solution(mesh):
    placed = (
        P(("slab", "pencil"), None),
        P(None, ("slab", "pencil")),
        P(None, ("slab", "pencil")),
        P(None, ("slab", "pencil")),
    )
    return jax.shard_map(
        shards,
        mesh=mesh,
        in_specs=placed,
        out_specs=P(None, None, "slab", "pencil"),
        check_vma=False,
    )
```

profile of v0, /device:TPU:0, one launch (start us, length us, event | category | flops | bytes accessed | tf_op | source)
XLA Modules:
  0.0 354.3 jit_solution(5115085824813003113)
XLA Ops:
  0.7 3.8 %sort.17 = (s32[256]{0:T(256)}, s32[256]{0:T(256)S(1)}) sort(s32[256]{0:T(256)} %bitcast.174, s32[256]{0:T(256)S(1)} %iota.109), dimensions={0}, to_apply=%region_0.0 | sort | flops 2048 | bytes 4096 | tf_op jit(solution)/shard_map/jit(argsort)/sort | solution.py:107
  4.6 2.0 gather_fusion
  8.4 4.3 %compare_select_fusion.1 = (s32[256,1]{0,1:T(1,128)S(1)}, s32[256,1]{0,1:T(1,128)S(1)}) fusion(s32[]{:T(128)} %bitcast.30, s32[]{:T(128)} %bitcast.31, s32[]{:T(128)} %bitcast.32, s32[]{:T(128)} %bitcast.33, s32[]{:T(128)} %bitcast.34, s32[]{:T(128)} %bitcast.36, s32[]{:T(128)} %bitcast.35, s32[256,1]{0,1:T(1,128)S(1)} %bitcast.236), kind=kLoop, calls=%fused_computation.186 | loop fusion | flops 3840 | bytes 3100 | tf_op jit(solution)/shard_map/gather | solution.py:112
  12.9 15.7 %select_subtract_fusion = s32[256]{0:T(256)S(1)} fusion(pred[256]{0:T(512)(128)(4,1)S(1)} %get-tuple-element.55, pred[256]{0:T(512)(128)(4,1)S(1)} %get-tuple-element.54, pred[256]{0:T(512)(128)(4,1)S(1)} %get-tuple-element.53, pred[256]{0:T(512)(128)(4,1)S(1)} %get-tuple-element.52, pred[256]{0:T(512)(128)(4,1)S(1)} %get-tuple-element.51, ...), kind=kLoop, calls=%fused_computation.220 | loop fusion | flops 6656 | bytes 8548 | tf_op jit(solution)/shard_map/sub | solution.py:112
  28.6 1.4 scatter_custom_fusion
  32.3 1.4 scatter_fusion
  34.7 7.3 %all-to-all-start = ((s32[8,1,384]{2,1,0:T(1,128)}), s32[8,1,384]{2,1,0:T(1,128)S(1)}, u32[]{:S(2)}, u32[]{:S(2)}) async-start(s32[8,1,384]{2,1,0:T(1,128)} %reshape.1138), calls=%async_computation | async-start | bytes 24576 | tf_op jit(solution)/shard_map/all_to_all | solution.py:128
  42.0 6.5 %all-to-all-done = s32[8,1,384]{2,1,0:T(1,128)S(1)} async-done(((s32[8,1,384]{2,1,0:T(1,128)}), s32[8,1,384]{2,1,0:T(1,128)S(1)}, u32[]{:S(2)}, u32[]{:S(2)}) %all-to-all-start) | async-done | bytes 12320 | tf_op jit(solution)/shard_map/all_to_all | solution.py:128
  50.4 3.2 all-to-all-start.1
  55.1 1.4 scatter_fusion.1
  57.5 3.3 all-to-all-start.2
  61.8 5.5 %all-to-all-done.2 = f32[8,1,640]{2,1,0:T(1,128)S(1)} async-done(((f32[8,1,640]{2,1,0:T(1,128)}), f32[8,1,640]{2,1,0:T(1,128)S(1)}, u32[]{:S(2)}, u32[]{:S(2)}) %all-to-all-start.2) | async-done | bytes 20512 | tf_op jit(solution)/shard_map/all_to_all | solution.py:135
  69.5 3.8 %all-to-all-start.3 = ((f32[4,1,1280]{2,1,0:T(1,128)}), f32[4,1,1280]{2,1,0:T(1,128)S(1)}, u32[]{:S(2)}, u32[]{:S(2)}) async-start(f32[4,1,1280]{2,1,0:T(1,128)} %reshape.1136), calls=%async_computation.3 | async-start | bytes 40960 | tf_op jit(solution)/shard_map/all_to_all | solution.py:134
  73.3 3.3 all-to-all-done.3
  79.1 2.6 broadcast_multiply_fusion
  81.7 4.9 %mul.941 = f32[1024,1080]{0,1:T(8,128)} reshape(f32[1024,8,135]{0,2,1:T(8,128)} %broadcast_multiply_fusion) | data formatting | bytes 8847360 | tf_op jit(solution)/shard_map/mul | solution.py:71
  86.6 4.8 %reshape.921 = f32[8,135,1024]{2,1,0:T(8,128)} reshape(f32[1080,1024]{1,0:T(8,128)} %bitcast.183) | data formatting | bytes 8847360 | tf_op jit(solution)/shard_map/reshape.869
  91.4 11.9 %fusion.25 = f32[1,8,135,512]{3,2,1,0:T(8,128)S(1)} fusion(f32[8,135,1024]{2,1,0:T(8,128)} %reshape.921, f32[1024]{0:T(1024)S(1)} %mul.1013, f32[1024]{0:T(1024)S(1)} %bitcast.222, s32[1024]{0:T(1024)S(1)} %get-tuple-element.99, f32[1024]{0:T(1024)S(1)} %bitcast.224, s32[1024]{0:T(1024)S(1)} %get-tuple-element.98, f32[1024]{0:T(1024)S(1)} %bitcast.226, ...), kind=kOutput, calls=%fused_computation.50 | convolution fusion | flops 6807355392 | bytes 6705152 | tf_op jit(solution)/shard_map/dot_general | solution.py:84
  103.3 9.7 %fusion.22 = f32[1,8,135,512]{3,2,1,0:T(8,128)S(1)} fusion(f32[8,135,1024]{2,1,0:T(8,128)S(1)} %copy-done.5, f32[1024]{0:T(1024)S(1)} %mul.1010, f32[1024]{0:T(1024)S(1)} %bitcast.223, s32[1024]{0:T(1024)S(1)} %get-tuple-element.99, f32[1024]{0:T(1024)S(1)} %bitcast.225, s32[1024]{0:T(1024)S(1)} %get-tuple-element.98, f32[1024]{0:T(1024)S(1)} %bitcast.227, ...), kind=kOutput, calls=%fused_computation.49 | convolution fusion | flops 6807355392 | bytes 6705152 | tf_op jit(solution)/shard_map/dot_general | solution.py:77
  113.0 2.5 fusion
  115.5 3.3 collective-permute-done
  118.9 2.0 scatter-add.9
  120.9 2.9 fusion.144
  123.8 8.4 %fusion.47 = f32[1024,512]{1,0:T(8,128)S(1)} fusion(f32[1024,512]{1,0:T(8,128)S(1)} %bitcast.188), kind=kOutput, calls=%fused_computation.71 | convolution fusion | flops 3225157632 | bytes 4194304 | tf_op jit(solution)/shard_map/dot_general | solution.py:95
  132.3 8.8 %fusion.152 = (f32[1024,512]{1,0:T(8,128)}, f32[1024,512]{1,0:T(8,128)S(1)}) fusion(f32[1024,512]{1,0:T(8,128)S(1)} %fusion.47, f32[1024,512]{1,0:T(8,128)S(1)} %bitcast.181), kind=kOutput, calls=%fused_computation.280 | convolution fusion | flops 3225681920 | bytes 8388608 | tf_op jit(solution)/shard_map/dot_general | solution.py:95
  141.0 7.9 %subtract_subtract_fusion = f32[1024,512]{1,0:T(8,128)S(1)} fusion(f32[1024,512]{1,0:T(8,128)S(1)} %fusion.47, f32[1024,512]{1,0:T(8,128)S(1)} %get-tuple-element.152, f32[1024,512]{1,0:T(8,128)S(1)} %bitcast.182, f32[1024,512]{1,0:T(8,128)S(1)} %bitcast.189), kind=kOutput, calls=%fused_computation.31 | convolution fusion | flops 3227254784 | bytes 10485760 | tf_op jit(solution)/shard_map/dot_general | solution.py:95
  149.0 1.9 copy.72
  150.9 3.6 %all-to-all-start.5 = ((f32[8,128,512]{1,0,2:T(8,128)}), f32[8,128,512]{1,0,2:T(8,128)S(1)}, u32[]{:S(2)}, u32[]{:S(2)}) async-start(f32[8,128,512]{1,0,2:T(8,128)} %copy.72), calls=%async_computation.5 | async-start | bytes 4194304 | tf_op jit(solution)/shard_map/all_to_all | solution.py:157
  154.5 2.9 copy.70
  157.4 22.7 %all-to-all-done.5 = f32[8,128,512]{1,0,2:T(8,128)S(1)} async-done(((f32[8,128,512]{1,0,2:T(8,128)}), f32[8,128,512]{1,0,2:T(8,128)S(1)}, u32[]{:S(2)}, u32[]{:S(2)}) %all-to-all-start.5) | async-done | bytes 2097184 | tf_op jit(solution)/shard_map/all_to_all | solution.py:157
  180.1 1.3 copy-done.3
  181.4 4.6 %all-to-all-start.4 = ((f32[8,128,512]{1,0,2:T(8,128)}), f32[8,128,512]{1,0,2:T(8,128)}, u32[]{:S(2)}, u32[]{:S(2)}) async-start(f32[8,128,512]{1,0,2:T(8,128)} %copy.70), calls=%async_computation.4 | async-start | bytes 4194304 | tf_op jit(solution)/shard_map/all_to_all | solution.py:156
  186.1 1.9 copy.73
  188.0 23.8 %all-to-all-done.4 = f32[8,128,512]{1,0,2:T(8,128)} async-done(((f32[8,128,512]{1,0,2:T(8,128)}), f32[8,128,512]{1,0,2:T(8,128)}, u32[]{:S(2)}, u32[]{:S(2)}) %all-to-all-start.4) | async-done | bytes 2097184 | tf_op jit(solution)/shard_map/all_to_all | solution.py:156
  211.8 2.9 copy.71
  214.7 9.0 %fusion.38 = f32[512,8,128]{2,0,1:T(8,128)S(1)} fusion(f32[8,512,128]{2,1,0:T(8,128)} %bitcast.184), kind=kOutput, calls=%fused_computation.60 | convolution fusion | flops 3225157632 | bytes 4194304 | tf_op jit(solution)/shard_map/nyx,ym->nmx/dot_general | solution.py:158
  223.6 9.2 %bitcast_subtract_fusion.1 = (f32[8,512,128]{2,1,0:T(8,128)S(1)}, f32[512,8,128]{2,0,1:T(8,128)}) fusion(f32[512,8,128]{2,0,1:T(8,128)S(1)} %fusion.38, f32[8,512,128]{2,1,0:T(8,128)S(1)} %bitcast.179), kind=kOutput, calls=%fused_computation.22 | convolution fusion | flops 3225681920 | bytes 8388608 | tf_op jit(solution)/shard_map/nyx,ym->nmx/dot_general | solution.py:165
  232.9 2.6 copy.74
  235.4 3.6 %all-to-all-start.6 = ((f32[8,512,128]{2,0,1:T(8,128)}), f32[8,512,128]{2,0,1:T(8,128)S(1)}, u32[]{:S(2)}, u32[]{:S(2)}) async-start(f32[8,512,128]{2,0,1:T(8,128)} %copy.74), calls=%async_computation.6 | async-start | bytes 4194304 | tf_op jit(solution)/shard_map/all_to_all | solution.py:182
  239.0 11.1 %fusion.7 = f32[8,512,128]{2,1,0:T(8,128)S(1)} fusion(f32[512,8,128]{2,0,1:T(8,128)} %get-tuple-element.154, f32[512,8,128]{2,0,1:T(8,128)} %copy-done.4, f32[8,512,128]{2,1,0:T(8,128)} %bitcast.185, f32[8,512,128]{2,1,0:T(8,128)} %bitcast.180), kind=kOutput, calls=%fused_computation.21 | convolution fusion | flops 3227254784 | bytes 10485760 | tf_op jit(solution)/shard_map/nyx,ym->nmx/dot_general | solution.py:172
  250.2 2.5 copy.76
  252.7 34.4 %all-to-all-done.6 = f32[8,512,128]{2,0,1:T(8,128)S(1)} async-done(((f32[8,512,128]{2,0,1:T(8,128)}), f32[8,512,128]{2,0,1:T(8,128)S(1)}, u32[]{:S(2)}, u32[]{:S(2)}) %all-to-all-start.6) | async-done | bytes 2097184 | tf_op jit(solution)/shard_map/all_to_all | solution.py:182
  288.4 4.6 %all-to-all-start.7 = ((f32[8,512,128]{2,0,1:T(8,128)}), f32[8,512,128]{2,0,1:T(8,128)}, u32[]{:S(2)}, u32[]{:S(2)}) async-start(f32[8,512,128]{2,0,1:T(8,128)} %copy.76), calls=%async_computation.7 | async-start | bytes 4194304 | tf_op jit(solution)/shard_map/all_to_all | solution.py:183
  293.0 3.6 %fusion.5 = f32[64,64,128]{2,0,1:T(8,128)S(1)} fusion(f32[8,8,64,128]{3,0,2,1:T(8,128)} %bitcast.177), kind=kOutput, calls=%fused_computation.18 | convolution fusion | flops 402714624 | bytes 4194304 | tf_op jit(solution)/shard_map/zyx,zm->myx/dot_general | solution.py:184
  296.6 44.2 %all-to-all-done.7 = f32[8,512,128]{2,0,1:T(8,128)} async-done(((f32[8,512,128]{2,0,1:T(8,128)}), f32[8,512,128]{2,0,1:T(8,128)}, u32[]{:S(2)}, u32[]{:S(2)}) %all-to-all-start.7) | async-done | bytes 2097184 | tf_op jit(solution)/shard_map/all_to_all | solution.py:183
  340.9 3.7 %fusion.1 = f32[64,64,128]{2,0,1:T(8,128)S(1)} fusion(f32[8,8,64,128]{3,0,2,1:T(8,128)} %bitcast.93), kind=kOutput, calls=%fused_computation.14 | convolution fusion | flops 402714624 | bytes 4194304 | tf_op jit(solution)/shard_map/zyx,zm->myx/dot_general | solution.py:191
  344.6 3.9 %subtract_bitcast_fusion = f32[1,64,64,128]{3,1,2,0:T(8,128)S(1)} fusion(f32[64,64,128]{2,0,1:T(8,128)S(1)} %fusion.1, f32[64,64,128]{2,0,1:T(8,128)S(1)} %fusion.5, f32[8,8,64,128]{3,0,2,1:T(8,128)} %bitcast.93, f32[8,8,64,128]{3,0,2,1:T(8,128)S(1)} %bitcast.178), kind=kOutput, calls=%fused_computation.27 | convolution fusion | flops 404295680 | bytes 10485760 | tf_op jit(solution)/shard_map/zyx,zm->myx/dot_general | solution.py:198
  349.5 4.4 %copy.78 = f32[2,64,64,128]{3,2,1,0:T(8,128)} copy(f32[2,64,64,128]{3,1,2,0:T(8,128)S(1)} %pad_maximum_fusion) | data formatting | bytes 8388608 | tf_op jit(solution)/shard_map/stack | solution.py:207
  (87 shorter events, 18.1 us)
Async XLA Ops:
  0.0 42.0 %copy-start.6 = (f32[3,256]{1,0:T(4,128)S(1)}, f32[3,256]{1,0:T(4,128)}, u32[]{:S(2)}) copy-start(f32[3,256]{1,0:T(4,128)} %param.10) | copy-start | bytes 9220
  0.0 42.0 %copy-start.7 = (f32[2,256]{1,0:T(2,128)S(1)}, f32[2,256]{1,0:T(2,128)}, u32[]{:S(2)}) copy-start(f32[2,256]{1,0:T(2,128)} %param.11) | copy-start | bytes 6148
  34.7 13.8 %all-to-all-start = ((s32[8,1,384]{2,1,0:T(1,128)}), s32[8,1,384]{2,1,0:T(1,128)S(1)}, u32[]{:S(2)}, u32[]{:S(2)}) async-start(s32[8,1,384]{2,1,0:T(1,128)} %reshape.1138), calls=%async_computation | async-start | bytes 24576 | tf_op jit(solution)/shard_map/all_to_all | solution.py:128
  50.4 7.1 %all-to-all-start.1 = ((s32[4,1,768]{2,1,0:T(1,128)}), s32[4,1,768]{2,1,0:T(1,128)S(1)}, u32[]{:S(2)}, u32[]{:S(2)}) async-start(s32[4,1,768]{2,1,0:T(1,128)} %reshape.1140), calls=%async_computation.1 | async-start | bytes 24576 | tf_op jit(solution)/shard_map/all_to_all | solution.py:127
  57.5 9.9 %all-to-all-start.2 = ((f32[8,1,640]{2,1,0:T(1,128)}), f32[8,1,640]{2,1,0:T(1,128)S(1)}, u32[]{:S(2)}, u32[]{:S(2)}) async-start(f32[8,1,640]{2,1,0:T(1,128)} %reshape.1134), calls=%async_computation.2 | async-start | bytes 40960 | tf_op jit(solution)/shard_map/all_to_all | solution.py:135
  69.5 7.1 %all-to-all-start.3 = ((f32[4,1,1280]{2,1,0:T(1,128)}), f32[4,1,1280]{2,1,0:T(1,128)S(1)}, u32[]{:S(2)}, u32[]{:S(2)}) async-start(f32[4,1,1280]{2,1,0:T(1,128)} %reshape.1136), calls=%async_computation.3 | async-start | bytes 40960 | tf_op jit(solution)/shard_map/all_to_all | solution.py:134
  91.4 11.9 %copy-start.5 = (f32[8,135,1024]{2,1,0:T(8,128)S(1)}, f32[8,135,1024]{2,1,0:T(8,128)}, u32[]{:S(2)}) copy-start(f32[8,135,1024]{2,1,0:T(8,128)} %reshape.921) | copy-start | bytes 13271044
  113.0 5.8 %collective-permute-start = (f32[2,8,7,512]{3,2,1,0:T(8,128)S(1)}, f32[2,8,7,512]{3,2,1,0:T(8,128)S(1)}, u32[]{:S(2)}, u32[]{:S(2)}) collective-permute-start(f32[2,8,7,512]{3,2,1,0:T(8,128)S(1)} %pad_maximum_fusion.1), channel_id=1, source_target_pairs={{3,0},{0,1},{1,2},{2,3},{7,4},{4,5},{5,6},{6,7},{11,8},{8,9},{9,10... | collective-permute-start | bytes 688136 | tf_op jit(solution)/shard_map/ppermute | solution.py:19
  150.9 29.2 %all-to-all-start.5 = ((f32[8,128,512]{1,0,2:T(8,128)}), f32[8,128,512]{1,0,2:T(8,128)S(1)}, u32[]{:S(2)}, u32[]{:S(2)}) async-start(f32[8,128,512]{1,0,2:T(8,128)} %copy.72), calls=%async_computation.5 | async-start | bytes 4194304 | tf_op jit(solution)/shard_map/all_to_all | solution.py:157
  180.1 1.3 copy-start.3
  181.4 30.3 %all-to-all-start.4 = ((f32[8,128,512]{1,0,2:T(8,128)}), f32[8,128,512]{1,0,2:T(8,128)}, u32[]{:S(2)}, u32[]{:S(2)}) async-start(f32[8,128,512]{1,0,2:T(8,128)} %copy.70), calls=%async_computation.4 | async-start | bytes 4194304 | tf_op jit(solution)/shard_map/all_to_all | solution.py:156
  188.0 35.6 %copy-start.2 = (f32[8,128,4,128]{3,1,2,0:T(8,128)}, f32[8,128,4,128]{3,1,2,0:T(8,128)S(1)}, u32[]{:S(2)}) copy-start(f32[8,128,4,128]{3,1,2,0:T(8,128)S(1)} %copy.73) | copy-start | bytes 6291460
  223.6 9.2 %copy-start.4 = (f32[512,8,128]{2,0,1:T(8,128)}, f32[512,8,128]{2,0,1:T(8,128)S(1)}, u32[]{:S(2)}) copy-start(f32[512,8,128]{2,0,1:T(8,128)S(1)} %fusion.38) | copy-start | bytes 6291460
  235.4 51.7 %all-to-all-start.6 = ((f32[8,512,128]{2,0,1:T(8,128)}), f32[8,512,128]{2,0,1:T(8,128)S(1)}, u32[]{:S(2)}, u32[]{:S(2)}) async-start(f32[8,512,128]{2,0,1:T(8,128)} %copy.74), calls=%async_computation.6 | async-start | bytes 4194304 | tf_op jit(solution)/shard_map/all_to_all | solution.py:182
  287.2 1.3 copy-start
  288.4 52.4 %all-to-all-start.7 = ((f32[8,512,128]{2,0,1:T(8,128)}), f32[8,512,128]{2,0,1:T(8,128)}, u32[]{:S(2)}, u32[]{:S(2)}) async-start(f32[8,512,128]{2,0,1:T(8,128)} %copy.76), calls=%async_computation.7 | async-start | bytes 4194304 | tf_op jit(solution)/shard_map/all_to_all | solution.py:183
  340.9 3.8 %copy-start.1 = (f32[8,512,128]{2,0,1:T(8,128)S(1)}, f32[8,512,128]{2,0,1:T(8,128)}, u32[]{:S(2)}) copy-start(f32[8,512,128]{2,0,1:T(8,128)} %copy-done) | copy-start | bytes 6291460
where the time goes:
time: 361 us; the launch traced here: 354 us
  waiting for transfers between devices  144 us (40%)
  matrix products  87.2 us (24%)
  local copies, waits for them, and re-layouts  53.4 us (15%)
  other arithmetic  34.9 us (10%)
  starting transfers between devices  34.1 us (9%)
    all_to_all x1, waiting for transfers between devices, shards(): lax.all_to_all(middle_imag, 'slab', split_axis=1, concat_axis=0, tiled=True)  44.2 us
    all_to_all x1, waiting for transfers between devices, shards(): lax.all_to_all(middle_real, 'slab', split_axis=1, concat_axis=0, tiled=True)  34.4 us
    dot_general x3, matrix products, product(): jnp.dot(left, right, precision=lax.Precision.HIGHEST, preferred_element_t...  25.1 us
    all_to_all x1, waiting for transfers between devices, shards(): lax.all_to_all(turned_real, 'pencil', split_axis=2, concat_axis=1, tiled=...  23.8 us
    all_to_all x1, waiting for transfers between devices, shards(): lax.all_to_all(turned_imag, 'pencil', split_axis=2, concat_axis=1, tiled=...  22.7 us
    sub x1, other arithmetic, shards(): jnp.arange(sample_count, dtype=jnp.int32) - starts[sorted_owner]  15.7 us
    dot_general x1, matrix products, spread_grid(): lax.dot_general(left_table, imag_right, numbers, precision=lax.Precision....  11.9 us
    dot_general x1, matrix products, shards(): jnp.einsum('nyx,ym->nmx', part_real + part_imag, both_y, precision=lax.Pr...  11.1 us
  transfers between devices with their start and end apart: 9, of which 8 were waited for; matrix products, arithmetic and copies ran while one was open for 8% of the time, Pallas kernels for 0%

commit v1 on v0

v1 whole, which is shorter than its diff:
```python
import math

import jax
import jax.numpy as jnp
import numpy as np
from jax import lax
from jax.experimental import pallas as pl
from jax.experimental.pallas import tpu as pltpu
from jax.sharding import PartitionSpec as P

NY = 512
NX = 512
PLANES = 8
TAPS = 8
WIDE = 2 * PLANES
LANES = 128
CHUNK = 256
BETA = 18.64
F32 = jnp.float32
BF16 = jnp.bfloat16


def series_terms():
    quarter = BETA * BETA / 4.0
    raw = [1.0]
    for order in range(1, 41):
        raw.append(raw[-1] * quarter / (order * order))
    total = sum(raw)
    return [value / total for value in raw]


TERMS = series_terms()


def window(gap):
    radicand = jnp.maximum(1.0 - gap * gap, 0.0)
    total = jnp.full(gap.shape, TERMS[40], F32)
    for order in range(39, -1, -1):
        total = total * radicand + TERMS[order]
    return total


def sin_cos(turns):
    half = (turns - jnp.floor(turns + 0.5)) * math.pi
    square = half * half
    sine = jnp.full(half.shape, 1.0 / math.factorial(13), F32)
    for order, sign in ((11, -1), (9, 1), (7, -1), (5, 1), (3, -1), (1, 1)):
        sine = sine * square + sign / math.factorial(order)
    sine = sine * half
    cosine = jnp.full(half.shape, 1.0 / math.factorial(12), F32)
    for order, sign in ((10, -1), (8, 1), (6, -1), (4, 1), (2, -1), (0, 1)):
        cosine = cosine * square + sign / math.factorial(order)
    return 2.0 * sine * cosine, 1.0 - 2.0 * sine * sine


def split(value):
    high = value.astype(BF16)
    low = (value - high.astype(F32)).astype(BF16)
    return high, low


def iota(shape, axis):
    return lax.broadcasted_iota(jnp.int32, shape, axis)


def order_kernel(n_pencil, tile_ref, tile_row_ref, cell_ref, frac_ref, value_ref, out_ref):
    count = tile_ref.shape[0]
    rows_per_tile = NY // n_pencil
    tile_row = tile_row_ref[...]
    slab_row = tile_row // n_pencil
    pencil_row = tile_row - slab_row * n_pencil
    slab_column = tile_ref[...] // n_pencil
    key_row = slab_row * count + iota((1, count), 1)
    key_column = slab_column * count + iota((count, 1), 0)
    rank = jnp.sum((key_row < key_column).astype(F32), axis=1, keepdims=True)
    place = (rank.astype(jnp.int32) == iota((count, count), 1)).astype(F32).astype(BF16)
    cells = cell_ref[...]
    numbers = jnp.concatenate(
        [
            (slab_row * PLANES + cells[0:1]).astype(F32),
            (pencil_row * rows_per_tile + cells[1:2]).astype(F32),
            cells[2:3].astype(F32),
            frac_ref[...],
            value_ref[...],
        ],
        axis=0,
    )
    high = numbers.astype(BF16).astype(F32)
    rest = numbers - high
    middle = rest.astype(BF16).astype(F32)
    low = rest - middle
    pieces = jnp.concatenate([high, middle, low], axis=0).astype(BF16)
    moved = jnp.dot(pieces, place, preferred_element_type=F32)
    out_ref[...] = (moved[0:8] + moved[8:16]) + moved[16:24]


def tap_table(rows, first, length):
    mode = first + iota((rows, 8), 0)
    sine, cosine = sin_cos((mode * iota((rows, 8), 1)).astype(F32) * (1.0 / length))
    table = jnp.concatenate([cosine, sine], axis=0)
    high = table.astype(BF16).astype(F32)
    return jnp.concatenate([high, table - high, high], axis=1).astype(BF16)


def tap_sum(table, weight):
    high = weight.astype(BF16).astype(F32)
    stacked = jnp.concatenate([high, high, weight - high], axis=0).astype(BF16)
    return jnp.dot(table, stacked, preferred_element_type=F32)


def phases(anchor, groups, first, length, value=None):
    outer = (first + 8 * iota((groups, 1), 0)).astype(F32)
    outer_sine, outer_cosine = sin_cos(anchor * outer * (1.0 / length))
    inner = iota((8, 1), 0).astype(F32)
    inner_sine, inner_cosine = sin_cos(anchor * inner * (1.0 / length))
    if value is not None:
        real, imag = value
        outer_cosine, outer_sine = (
            outer_cosine * real - outer_sine * imag,
            outer_cosine * imag + outer_sine * real,
        )
    reals, imags = [], []
    for a in range(groups):
        c, s = outer_cosine[a : a + 1], outer_sine[a : a + 1]
        reals.append(c * inner_cosine - s * inner_sine)
        imags.append(c * inner_sine + s * inner_cosine)
    return reals, imags


def spread_kernel(
    n_slab,
    modes_y,
    modes_x,
    samples_ref,
    depth_table_ref,
    out_ref,
    ends_ref,
    ends_smem,
    packed_ref,
    grid_ref,
    b_ref,
    high_ref,
    low_ref,
    right_ref,
    table_y_ref,
    table_x_ref,
    turned_ref,
    copy_sem,
    out_sem,
):
    devices = samples_ref.shape[0]
    depth = n_slab * PLANES
    first_y = lax.axis_index("slab") * modes_y
    first_x = lax.axis_index("pencil") * modes_x
    lane = iota((8, LANES), 1)

    slab_of = samples_ref[:, 0, :]
    column = iota((devices, LANES), 1)

    def count(s, ends):
        below = (slab_of < ((s + 1) * PLANES).astype(F32)).astype(F32)
        return jnp.where(column == s + 1, jnp.sum(below, axis=1, keepdims=True), ends)

    ends = lax.fori_loop(0, n_slab, count, jnp.zeros((devices, LANES), F32))
    ends_ref[...] = ends.astype(jnp.int32)
    copy = pltpu.make_async_copy(ends_ref, ends_smem, copy_sem)
    copy.start()
    table_y_ref[...] = tap_table(modes_y, first_y, NY)
    table_x_ref[...] = tap_table(modes_x, first_x, NX)
    grid_ref[...] = jnp.zeros_like(grid_ref)
    copy.wait()

    def slab_step(s, carry):
        def pack(d, state):
            offset, first, second = state
            begin = ends_smem[d, s]
            size = ends_smem[d, s + 1] - begin
            shift = (offset - begin) & (CHUNK - 1)
            low_shift = shift & (LANES - 1)
            left = pltpu.roll(samples_ref[d, :, 0:LANES], low_shift, 1)
            right = pltpu.roll(samples_ref[d, :, LANES : 2 * LANES], low_shift, 1)
            wrapped = lane < low_shift
            one = jnp.where(wrapped, right, left)
            two = jnp.where(wrapped, left, right)
            swap = shift >= LANES
            one, two = jnp.where(swap, two, one), jnp.where(swap, one, two)
            inside = offset & (CHUNK - 1)
            new_first = jnp.where(lane >= inside, one, first)
            new_second = jnp.where(lane + LANES >= inside, two, second)
            at = offset >> 8
            packed_ref[at, :, 0:LANES] = new_first
            packed_ref[at, :, LANES : 2 * LANES] = new_second
            crossed = inside + size >= CHUNK
            return (
                offset + size,
                jnp.where(crossed, one, new_first),
                jnp.where(crossed, two, new_second),
            )

        empty = jnp.zeros((8, LANES), F32)
        total, first, second = lax.fori_loop(
            0, devices, pack, (jnp.int32(0), empty, empty), unroll=8
        )
        packed_ref[total >> 8, :, 0:LANES] = first
        packed_ref[total >> 8, :, LANES : 2 * LANES] = second
        base = pl.multiple_of(s * PLANES, PLANES)

        def chunk_step(c, carry):
            numbers = packed_ref[c]
            anchor_z, anchor_y, anchor_x = numbers[0:1], numbers[1:2], numbers[2:3]
            frac_z, frac_y, frac_x = numbers[3:4], numbers[4:5], numbers[5:6]
            valid = iota((1, CHUNK), 1) + c * CHUNK < total
            real = jnp.where(valid, numbers[6:7], 0.0)
            imag = jnp.where(valid, numbers[7:8], 0.0)
            tap_z = iota((WIDE, CHUNK), 0).astype(F32) - (anchor_z - (s * PLANES).astype(F32))
            tap = iota((TAPS, CHUNK), 0).astype(F32) - 3.0
            weights = window(
                jnp.concatenate([tap_z - 3.0 - frac_z, tap - frac_y, tap - frac_x], axis=0) * 0.25
            )
            weight_z = jnp.where((tap_z >= 0.0) & (tap_z < TAPS), weights[0:WIDE], 0.0)
            sum_y = tap_sum(table_y_ref[...], weights[WIDE : WIDE + TAPS])
            sum_x = tap_sum(table_x_ref[...], weights[WIDE + TAPS : WIDE + 2 * TAPS])
            reals, imags = phases(anchor_x, modes_x // 8, first_x, NX, (real, imag))
            for a in range(modes_x // 8):
                sr = sum_x[8 * a : 8 * a + 8]
                si = sum_x[modes_x + 8 * a : modes_x + 8 * a + 8]
                b_ref[8 * a : 8 * a + 8] = reals[a] * sr - imags[a] * si
                b_ref[modes_x + 8 * a : modes_x + 8 * a + 8] = reals[a] * si + imags[a] * sr
            high, low = split(b_ref[0 : 2 * modes_x])
            right_ref[:, 0:CHUNK] = high
            right_ref[:, CHUNK : 2 * CHUNK] = low
            right_ref[:, 2 * CHUNK : 3 * CHUNK] = high
            reals, imags = phases(anchor_y, modes_y // 8, first_y, NY)
            for a in range(modes_y // 8):
                sr = sum_y[8 * a : 8 * a + 8]
                si = sum_y[modes_y + 8 * a : modes_y + 8 * a + 8]
                block = reals[a] * sr - imags[a] * si, reals[a] * si + imags[a] * sr
                for part in range(2):
                    for b in range(8):
                        m = part * modes_y + 8 * a + b
                        high, low = split(weight_z * block[part][b : b + 1])
                        high_ref[m * WIDE : (m + 1) * WIDE] = high
                        low_ref[m * WIDE : (m + 1) * WIDE] = low
            step = min(512, 2 * modes_y * WIDE)
            for begin in range(0, 2 * modes_y * WIDE, step):
                high = high_ref[begin : begin + step]
                left = jnp.concatenate([high, high, low_ref[begin : begin + step]], axis=1)
                added = lax.dot_general(
                    left, right_ref[...], (((1,), (1,)), ((), ())), preferred_element_type=F32
                )
                m0, m1 = begin // WIDE, (begin + step) // WIDE
                grid_ref[m0:m1, pl.ds(base, WIDE), :] += added.reshape(m1 - m0, WIDE, 2 * modes_x)
            return carry

        return lax.fori_loop(0, (total + CHUNK - 1) // CHUNK, chunk_step, carry)

    lax.fori_loop(0, n_slab, slab_step, 0)
    grid_ref[:, 0:PLANES, :] += grid_ref[:, depth : depth + PLANES, :]

    pitch = turned_ref.shape[0] // (2 * depth)

    def turn(pair, carry):
        highs, lows = [], []
        for k in range(2):
            y = 2 * pair + k
            of_real = grid_ref[y, 0:depth, :]
            of_imag = grid_ref[modes_y + y, 0:depth, :]
            both = jnp.concatenate(
                [
                    of_real[:, :modes_x] - of_imag[:, modes_x:],
                    of_real[:, modes_x:] + of_imag[:, :modes_x],
                ],
                axis=0,
            )
            high, low = split(both)
            highs.append(high)
            lows.append(low)
        high = jnp.concatenate(highs, axis=1)
        low = jnp.concatenate(lows, axis=1)
        done = jnp.dot(
            depth_table_ref[...],
            jnp.concatenate([high, low, high], axis=0),
            preferred_element_type=F32,
        )
        for k in range(2):
            turned_ref[pl.ds(2 * pair + k, 2 * depth, stride=pitch), :] = done[
                :, k * modes_x : (k + 1) * modes_x
            ]
        return carry

    lax.fori_loop(0, modes_y // 2, turn, 0)

    def send(m, carry):
        pltpu.make_async_copy(
            turned_ref.at[pl.ds(pl.multiple_of(m * pitch, 8), modes_y)], out_ref.at[m], out_sem
        ).start()
        return carry

    lax.fori_loop(0, 2 * depth, send, 0)
    pltpu.make_async_copy(out_ref, out_ref, out_sem).wait()


def depth_table(depth):
    scale = 1.0 / math.sqrt(depth * NY * NX)
    index = np.arange(depth)
    angle = 2.0 * np.pi * (index[:, None] * index[None, :] % depth) / depth
    cosine, sine = np.cos(angle) * scale, np.sin(angle) * scale
    table = np.block([[cosine, -sine], [sine, cosine]]).astype(np.float32)
    high = table.astype(jnp.bfloat16)
    low = (table - high.astype(np.float32)).astype(jnp.bfloat16)
    return np.concatenate([high, high, low], axis=1)


def shards(sample_tile, sample_cell, sample_frac, sample_value):
    n_slab = lax.axis_size("slab")
    n_pencil = lax.axis_size("pencil")
    devices = n_slab * n_pencil
    samples = sample_tile.shape[0]
    depth = n_slab * PLANES
    modes_y = NY // n_slab
    modes_x = NX // n_pencil
    vmem = pl.BlockSpec(memory_space=pltpu.VMEM)
    own = pl.pallas_call(
        lambda *refs: order_kernel(n_pencil, *refs),
        out_shape=jax.ShapeDtypeStruct((8, samples), F32),
        in_specs=[vmem] * 5,
        out_specs=vmem,
        name="order",
    )(sample_tile, sample_tile.reshape(1, samples), sample_cell, sample_frac, sample_value)
    everyone = lax.all_to_all(
        jnp.broadcast_to(own[None], (devices, 8, samples)),
        ("slab", "pencil"),
        split_axis=0,
        concat_axis=0,
        tiled=False,
    )
    pitch = modes_y + 8
    volume = pl.pallas_call(
        lambda *refs: spread_kernel(n_slab, modes_y, modes_x, *refs),
        out_shape=jax.ShapeDtypeStruct((2 * depth, modes_y, modes_x), F32),
        in_specs=[vmem, vmem],
        out_specs=pl.BlockSpec(memory_space=pl.ANY),
        scratch_shapes=[
            pltpu.VMEM((devices, LANES), jnp.int32),
            pltpu.SMEM((devices, LANES), jnp.int32),
            pltpu.VMEM((devices * samples // CHUNK + 1, 8, CHUNK), F32),
            pltpu.VMEM((2 * modes_y, depth + PLANES, 2 * modes_x), F32),
            pltpu.VMEM((2 * modes_x, CHUNK), F32),
            pltpu.VMEM((2 * modes_y * WIDE, CHUNK), BF16),
            pltpu.VMEM((2 * modes_y * WIDE, CHUNK), BF16),
            pltpu.VMEM((2 * modes_x, 3 * CHUNK), BF16),
            pltpu.VMEM((2 * modes_y, 24), BF16),
            pltpu.VMEM((2 * modes_x, 24), BF16),
            pltpu.VMEM((2 * depth * pitch, modes_x), F32),
            pltpu.SemaphoreType.DMA,
            pltpu.SemaphoreType.DMA,
        ],
        name="spread",
    )(everyone, jnp.asarray(depth_table(depth)))
    return volume.reshape(2, depth, modes_y, modes_x)


def solution(mesh):
    placed = (
        P(("slab", "pencil"), None),
        P(None, ("slab", "pencil")),
        P(None, ("slab", "pencil")),
        P(None, ("slab", "pencil")),
    )
    return jax.shard_map(
        shards,
        mesh=mesh,
        in_specs=placed,
        out_specs=P(None, None, "slab", "pencil"),
        check_vma=False,
    )
```

time: 361 us -> 84.3 us (0.23); the launches traced: 354 us -> 84.1 us
  waiting for transfers between devices: 144 us -> 0 us
  matrix products: 87.2 us -> 0 us
  Pallas kernels: 0 us -> 64.1 us
  local copies, waits for them, and re-layouts: 53.4 us -> 2.19 us
  other arithmetic: 34.9 us -> 0 us
  starting transfers between devices: 34.1 us -> 0 us
  blocking collectives: 0 us -> 17.8 us
    all_to_all x8 -> x0, waiting for transfers between devices: 141 us -> none  [the longest x1 44.2 us: shards(): lax.all_to_all(middle_imag, 'slab', split_axis=1, concat_axis=0, tiled=True)]
    dot_general x11 -> x0, matrix products: 87.2 us -> none  [the longest x3 25.1 us: product(): jnp.dot(left, right, precision=lax.Precision.HIGHEST, preferred_element_t...]
    pallas_call x0 -> x2, Pallas kernels: none -> 64.1 us  [the longest x1 62.2 us: shards(): pl.pallas_call(lambda *refs: spread_kernel(n_slab, modes_y, modes_x, *ref...]
    all_to_all x8 -> x0, starting transfers between devices: 34.1 us -> none  [the longest x1 7.28 us: shards(): lax.all_to_all(cell_buffer, 'slab', split_axis=1, concat_axis=1, tiled=True)]
    all_to_all x0 -> x1, blocking collectives: none -> 17.8 us  [shards(): lax.all_to_all(jnp.broadcast_to(own[None], (devices, 8, samples)), ('slab...]
    sub x3 -> x0, other arithmetic: 15.7 us -> none  [the longest x1 15.7 us: shards(): jnp.arange(sample_count, dtype=jnp.int32) - starts[sorted_owner]]
    another operation x3 -> x0, local copies, waits for them, and re-layouts: 9.36 us -> none
    scatter x5 -> x0, local copies, waits for them, and re-layouts: 6.71 us -> none  [the longest x2 2.66 us: shards(): cell_buffer.at[:, first_slot].set(sample_cell).at[:, second_slot]]
  transfers between devices with their start and end apart: 9 -> 0, of which waited for: 8 -> 0; matrix products, arithmetic and copies ran while one was open for 8% -> 0% of each run, Pallas kernels for 0% -> 0%
where the time goes in v1:
time: 84.3 us; the launch traced here: 84.1 us
  Pallas kernels  64.1 us (76%)
  blocking collectives  17.8 us (21%)
  local copies, waits for them, and re-layouts  2.19 us (3%)
    pallas_call x1, Pallas kernels, shards(): pl.pallas_call(lambda *refs: spread_kernel(n_slab, modes_y, modes_x, *ref...  62.2 us
    all_to_all x1, blocking collectives, shards(): lax.all_to_all(jnp.broadcast_to(own[None], (devices, 8, samples)), ('slab...  17.8 us
    pallas_call x1, Pallas kernels, shards(): pl.pallas_call(lambda *refs: order_kernel(n_pencil, *refs), out_shape=jax...  1.89 us

profile of v1, /device:TPU:0, one launch (start us, length us, event | category | flops | bytes accessed | tf_op | source)
XLA Modules:
  0.0 84.1 jit_solution(7390752276688115424)
XLA Ops:
  0.0 1.5 %copy.6.refs_0_ = s32[256,1]{1,0:T(8,128)} copy(s32[256,1]{0,1:T(1,128)} %param.5) | data formatting | bytes 2048 | tf_op args[0]
  1.5 1.9 %order.1 = f32[8,256]{1,0:T(8,128)} custom-call(s32[256,1]{1,0:T(8,128)} %copy.6.refs_0_, s32[1,256]{1,0:T(1,128)} %bitcast.2, s32[3,256]{1,0:T(4,128)} %refs_2_.1, f32[3,256]{1,0:T(4,128)} %refs_3_.1, f32[2,256]{1,0:T(2,128)} %refs_4_.1), custom_call_target="tpu_custom_call" | custom-call | tf_op jit(solution)/shard_map/order/pallas_call | solution.py:323
  3.4 0.7 broadcast_in_dim.2
  4.1 17.8 %all_to_all.5.refs_0_ = f32[32,8,256]{2,1,0:T(8,128)} all-to-all(f32[32,8,256]{2,1,0:T(8,128)S(1)} %broadcast_in_dim.2), channel_id=1, replica_groups=mesh['slab'=8,'pencil'=4] {'slab','pencil'}, dimensions={0} | all-to-all | bytes 524288 | tf_op jit(solution)/shard_map/all_to_all | solution.py:330
  21.9 62.2 %spread.1 = f32[128,64,128]{2,1,0:T(8,128)} custom-call(f32[32,8,256]{2,1,0:T(8,128)} %all_to_all.5.refs_0_, bf16[128,384]{1,0:T(8,128)(2,1)} %constant.2.clone.refs_1_), custom_call_target="tpu_custom_call" | custom-call | tf_op jit(solution)/shard_map/spread/pallas_call | solution.py:338

commit v2 on v1

v2 whole, which is shorter than its diff:
```python
import math

import jax
import jax.numpy as jnp
import numpy as np
from jax import lax
from jax.experimental import pallas as pl
from jax.experimental.pallas import tpu as pltpu
from jax.sharding import PartitionSpec as P

NY = 512
NX = 512
PLANES = 8
TAPS = 8
WIDE = 2 * PLANES
LANES = 128
CHUNK = 256
STEP = 256
BETA = 18.64
F32 = jnp.float32
BF16 = jnp.bfloat16


def series_terms():
    quarter = BETA * BETA / 4.0
    raw = [1.0]
    for order in range(1, 41):
        raw.append(raw[-1] * quarter / (order * order))
    total = sum(raw)
    return [value / total for value in raw]


TERMS = series_terms()


def window(gap):
    radicand = jnp.maximum(1.0 - gap * gap, 0.0)
    total = jnp.full(gap.shape, TERMS[40], F32)
    for order in range(39, -1, -1):
        total = total * radicand + TERMS[order]
    return total


def sin_cos(turns):
    half = (turns - jnp.floor(turns + 0.5)) * math.pi
    square = half * half
    sine = jnp.full(half.shape, 1.0 / math.factorial(13), F32)
    for order, sign in ((11, -1), (9, 1), (7, -1), (5, 1), (3, -1), (1, 1)):
        sine = sine * square + sign / math.factorial(order)
    sine = sine * half
    cosine = jnp.full(half.shape, 1.0 / math.factorial(12), F32)
    for order, sign in ((10, -1), (8, 1), (6, -1), (4, 1), (2, -1), (0, 1)):
        cosine = cosine * square + sign / math.factorial(order)
    return 2.0 * sine * cosine, 1.0 - 2.0 * sine * sine


def split(value):
    high = value.astype(BF16)
    low = (value - high.astype(F32)).astype(BF16)
    return high, low


def iota(shape, axis):
    return lax.broadcasted_iota(jnp.int32, shape, axis)


def order_kernel(n_pencil, tile_ref, cell_ref, frac_ref, value_ref, out_ref):
    count = tile_ref.shape[1]
    rows_per_tile = NY // n_pencil
    tile_row = tile_ref[...]
    slab_row = tile_row // n_pencil
    pencil_row = tile_row - slab_row * n_pencil
    key_row = (slab_row * count + iota((1, count), 1)).astype(F32)
    square = (count, count)
    key_column = jnp.sum(
        jnp.where(iota(square, 0) == iota(square, 1), key_row, 0.0), axis=1, keepdims=True
    )
    rank = jnp.sum((key_row < key_column).astype(F32), axis=1, keepdims=True)
    place = (rank.astype(jnp.int32) == iota(square, 1)).astype(F32).astype(BF16)
    cells = cell_ref[...]
    numbers = jnp.concatenate(
        [
            (slab_row * PLANES + cells[0:1]).astype(F32),
            (pencil_row * rows_per_tile + cells[1:2]).astype(F32),
            cells[2:3].astype(F32),
            frac_ref[...],
            value_ref[...],
        ],
        axis=0,
    )
    high = numbers.astype(BF16).astype(F32)
    rest = numbers - high
    middle = rest.astype(BF16).astype(F32)
    low = rest - middle
    pieces = jnp.concatenate([high, middle, low], axis=0).astype(BF16)
    moved = jnp.dot(pieces, place, preferred_element_type=F32)
    out_ref[...] = jnp.broadcast_to(
        ((moved[0:8] + moved[8:16]) + moved[16:24])[None], out_ref.shape
    )


def tap_table(rows, first, length):
    mode = first + iota((rows, 8), 0)
    sine, cosine = sin_cos((mode * iota((rows, 8), 1)).astype(F32) * (1.0 / length))
    table = jnp.concatenate([cosine, sine], axis=0)
    high = table.astype(BF16).astype(F32)
    return jnp.concatenate([high, table - high, high], axis=1).astype(BF16)


def tap_sum(table, weight):
    high = weight.astype(BF16).astype(F32)
    stacked = jnp.concatenate([high, high, weight - high], axis=0).astype(BF16)
    return jnp.dot(table, stacked, preferred_element_type=F32)


def phases(anchor, groups, first, length, value=None):
    outer = (first + 8 * iota((groups, 1), 0)).astype(F32)
    outer_sine, outer_cosine = sin_cos(anchor * outer * (1.0 / length))
    inner = iota((8, 1), 0).astype(F32)
    inner_sine, inner_cosine = sin_cos(anchor * inner * (1.0 / length))
    if value is not None:
        real, imag = value
        outer_cosine, outer_sine = (
            outer_cosine * real - outer_sine * imag,
            outer_cosine * imag + outer_sine * real,
        )
    reals, imags = [], []
    for a in range(groups):
        c, s = outer_cosine[a : a + 1], outer_sine[a : a + 1]
        reals.append(c * inner_cosine - s * inner_sine)
        imags.append(c * inner_sine + s * inner_cosine)
    return reals, imags


def spread_kernel(
    n_slab,
    modes_y,
    modes_x,
    samples_ref,
    depth_table_ref,
    out_ref,
    ends_ref,
    ends_smem,
    slab_smem,
    size_smem,
    packed_ref,
    grid_ref,
    left_a,
    left_b,
    weight_a,
    weight_b,
    right_a,
    right_b,
    table_y_ref,
    table_x_ref,
    turned_ref,
    copy_sem,
    out_sem,
):
    devices = samples_ref.shape[0]
    depth = n_slab * PLANES
    first_y = lax.axis_index("slab") * modes_y
    first_x = lax.axis_index("pencil") * modes_x
    lane = iota((8, LANES), 1)

    slab_of = samples_ref[:, 0, :]
    column = iota((devices, LANES), 1)

    def count(s, ends):
        below = (slab_of < ((s + 1) * PLANES).astype(F32)).astype(F32)
        return jnp.where(column == s + 1, jnp.sum(below, axis=1, keepdims=True), ends)

    ends = lax.fori_loop(0, n_slab, count, jnp.zeros((devices, LANES), F32))
    ends_ref[...] = ends.astype(jnp.int32)
    copy = pltpu.make_async_copy(ends_ref, ends_smem, copy_sem)
    copy.start()
    table_y_ref[...] = tap_table(modes_y, first_y, NY)
    table_x_ref[...] = tap_table(modes_x, first_x, NX)
    grid_ref[...] = jnp.zeros_like(grid_ref)
    copy.wait()

    def slab_step(s, chunks):
        def pack(d, state):
            offset, first, second = state
            begin = ends_smem[d, s]
            size = ends_smem[d, s + 1] - begin
            shift = (offset - begin) & (CHUNK - 1)
            low_shift = shift & (LANES - 1)
            left = pltpu.roll(samples_ref[d, :, 0:LANES], low_shift, 1)
            right = pltpu.roll(samples_ref[d, :, LANES : 2 * LANES], low_shift, 1)
            wrapped = lane < low_shift
            one = jnp.where(wrapped, right, left)
            two = jnp.where(wrapped, left, right)
            swap = shift >= LANES
            one, two = jnp.where(swap, two, one), jnp.where(swap, one, two)
            inside = offset & (CHUNK - 1)
            new_first = jnp.where(lane >= inside, one, first)
            new_second = jnp.where(lane + LANES >= inside, two, second)
            at = offset >> 8
            packed_ref[at, :, 0:LANES] = new_first
            packed_ref[at, :, LANES : 2 * LANES] = new_second
            crossed = inside + size >= CHUNK
            return (
                offset + size,
                jnp.where(crossed, one, new_first),
                jnp.where(crossed, two, new_second),
            )

        empty = jnp.zeros((8, LANES), F32)
        begin = chunks * CHUNK
        end, first, second = lax.fori_loop(0, devices, pack, (begin, empty, empty), unroll=8)
        packed_ref[end >> 8, :, 0:LANES] = first
        packed_ref[end >> 8, :, LANES : 2 * LANES] = second
        more = (end - begin + CHUNK - 1) >> 8

        def note(c, carry):
            slab_smem[chunks + c] = s
            size_smem[chunks + c] = end - begin - c * CHUNK
            return carry

        lax.fori_loop(0, more, note, 0)
        return chunks + more

    chunks = lax.fori_loop(0, n_slab, slab_step, jnp.int32(0))

    def prepare(c, left_ref, weight_ref, right_ref):
        c = jnp.minimum(c, chunks - 1)
        numbers = packed_ref[c]
        anchor_z, anchor_y, anchor_x = numbers[0:1], numbers[1:2], numbers[2:3]
        frac_z, frac_y, frac_x = numbers[3:4], numbers[4:5], numbers[5:6]
        valid = iota((1, CHUNK), 1) < size_smem[c]
        real = jnp.where(valid, numbers[6:7], 0.0)
        imag = jnp.where(valid, numbers[7:8], 0.0)
        plane = (slab_smem[c] * PLANES).astype(F32)
        tap_z = iota((WIDE, CHUNK), 0).astype(F32) - (anchor_z - plane)
        tap = iota((TAPS, CHUNK), 0).astype(F32) - 3.0
        weights = window(
            jnp.concatenate([tap_z - 3.0 - frac_z, tap - frac_y, tap - frac_x], axis=0) * 0.25
        )
        weight_ref[...] = jnp.where((tap_z >= 0.0) & (tap_z < TAPS), weights[0:WIDE], 0.0)
        sum_y = tap_sum(table_y_ref[...], weights[WIDE : WIDE + TAPS])
        sum_x = tap_sum(table_x_ref[...], weights[WIDE + TAPS : WIDE + 2 * TAPS])
        reals, imags = phases(anchor_x, modes_x // 8, first_x, NX, (real, imag))
        for a in range(0, modes_x // 8, 2):
            of_real, of_imag = [], []
            for k in (a, a + 1):
                sr = sum_x[8 * k : 8 * k + 8]
                si = sum_x[modes_x + 8 * k : modes_x + 8 * k + 8]
                of_real.append(reals[k] * sr - imags[k] * si)
                of_imag.append(reals[k] * si + imags[k] * sr)
            for part, pieces in ((0, of_real), (1, of_imag)):
                high, low = split(jnp.concatenate(pieces, axis=0))
                begin = part * modes_x + 8 * a
                right_ref[begin : begin + 16, 0:CHUNK] = high
                right_ref[begin : begin + 16, CHUNK : 2 * CHUNK] = low
        reals, imags = phases(anchor_y, modes_y // 8, first_y, NY)
        for a in range(modes_y // 8):
            sr = sum_y[8 * a : 8 * a + 8]
            si = sum_y[modes_y + 8 * a : modes_y + 8 * a + 8]
            left_ref[8 * a : 8 * a + 8] = reals[a] * sr - imags[a] * si
            left_ref[modes_y + 8 * a : modes_y + 8 * a + 8] = reals[a] * si + imags[a] * sr

    def gather(c, left_ref, weight_ref, right_ref):
        base = pl.multiple_of(slab_smem[c] * PLANES, PLANES)
        step = min(STEP // WIDE, 2 * modes_y)
        right = jnp.concatenate([right_ref[...], right_ref[:, 0:CHUNK]], axis=1)
        weight_z = weight_ref[...]
        for begin in range(0, 2 * modes_y, step):
            highs, lows = [], []
            for m in range(begin, begin + step):
                high, low = split(weight_z * left_ref[m : m + 1])
                highs.append(high)
                lows.append(low)
            high = jnp.concatenate(highs, axis=0)
            left = jnp.concatenate([high, high, jnp.concatenate(lows, axis=0)], axis=1)
            added = lax.dot_general(
                left, right, (((1,), (1,)), ((), ())), preferred_element_type=F32
            )
            grid_ref[begin : begin + step, pl.ds(base, WIDE), :] += added.reshape(
                step, WIDE, 2 * modes_x
            )

    prepare(0, left_a, weight_a, right_a)

    def two_chunks(pair, carry):
        c = 2 * pair
        gather(c, left_a, weight_a, right_a)
        prepare(c + 1, left_b, weight_b, right_b)

        @pl.when(c + 1 < chunks)
        def _():
            gather(c + 1, left_b, weight_b, right_b)
            prepare(c + 2, left_a, weight_a, right_a)

        return carry

    lax.fori_loop(0, (chunks + 1) >> 1, two_chunks, 0)
    grid_ref[:, 0:PLANES, :] += grid_ref[:, depth : depth + PLANES, :]

    groups = modes_y // 8

    def out_copy(group, slot):
        return pltpu.make_async_copy(
            turned_ref.at[slot],
            out_ref.at[:, pl.ds(pl.multiple_of(8 * group, 8), 8), :],
            out_sem.at[slot],
        )

    def turn(group, carry):
        slot = group & 1

        @pl.when(group >= 2)
        def _():
            out_copy(group - 2, slot).wait()

        rows_ref = turned_ref.at[slot].reshape(2 * depth * 8, modes_x)
        for pair in range(4):
            highs, lows = [], []
            for k in range(2):
                y = 8 * group + 2 * pair + k
                of_real = grid_ref[y, 0:depth, :]
                of_imag = grid_ref[modes_y + y, 0:depth, :]
                both = jnp.concatenate(
                    [
                        of_real[:, :modes_x] - of_imag[:, modes_x:],
                        of_real[:, modes_x:] + of_imag[:, :modes_x],
                    ],
                    axis=0,
                )
                high, low = split(both)
                highs.append(high)
                lows.append(low)
            high = jnp.concatenate(highs, axis=1)
            low = jnp.concatenate(lows, axis=1)
            done = jnp.dot(
                depth_table_ref[...],
                jnp.concatenate([high, low, high], axis=0),
                preferred_element_type=F32,
            )
            for k in range(2):
                rows_ref[pl.ds(2 * pair + k, 2 * depth, stride=8), :] = done[
                    :, k * modes_x : (k + 1) * modes_x
                ]
        out_copy(group, slot).start()
        return carry

    lax.fori_loop(0, groups, turn, 0)
    for back in range(min(2, groups), 0, -1):
        out_copy(groups - back, (groups - back) & 1).wait()


def depth_table(depth):
    scale = 1.0 / math.sqrt(depth * NY * NX)
    index = np.arange(depth)
    angle = 2.0 * np.pi * (index[:, None] * index[None, :] % depth) / depth
    cosine, sine = np.cos(angle) * scale, np.sin(angle) * scale
    table = np.block([[cosine, -sine], [sine, cosine]]).astype(np.float32)
    high = table.astype(jnp.bfloat16)
    low = (table - high.astype(np.float32)).astype(jnp.bfloat16)
    return np.concatenate([high, high, low], axis=1)


def shards(sample_tile, sample_cell, sample_frac, sample_value):
    n_slab = lax.axis_size("slab")
    n_pencil = lax.axis_size("pencil")
    devices = n_slab * n_pencil
    samples = sample_tile.shape[0]
    depth = n_slab * PLANES
    modes_y = NY // n_slab
    modes_x = NX // n_pencil
    vmem = pl.BlockSpec(memory_space=pltpu.VMEM)
    sent = pl.pallas_call(
        lambda *refs: order_kernel(n_pencil, *refs),
        out_shape=jax.ShapeDtypeStruct((devices, 8, samples), F32),
        in_specs=[vmem] * 4,
        out_specs=vmem,
        name="order",
    )(sample_tile.reshape(1, samples), sample_cell, sample_frac, sample_value)
    everyone = lax.all_to_all(
        sent, ("slab", "pencil"), split_axis=0, concat_axis=0, tiled=False
    )
    most = devices * samples // CHUNK + n_slab
    left = pltpu.VMEM((2 * modes_y, CHUNK), F32)
    weight = pltpu.VMEM((WIDE, CHUNK), F32)
    right = pltpu.VMEM((2 * modes_x, 2 * CHUNK), BF16)
    volume = pl.pallas_call(
        lambda *refs: spread_kernel(n_slab, modes_y, modes_x, *refs),
        out_shape=jax.ShapeDtypeStruct((2 * depth, modes_y, modes_x), F32),
        in_specs=[vmem, vmem],
        out_specs=pl.BlockSpec(memory_space=pl.ANY),
        scratch_shapes=[
            pltpu.VMEM((devices, LANES), jnp.int32),
            pltpu.SMEM((devices, LANES), jnp.int32),
            pltpu.SMEM((most,), jnp.int32),
            pltpu.SMEM((most,), jnp.int32),
            pltpu.VMEM((most + 1, 8, CHUNK), F32),
            pltpu.VMEM((2 * modes_y, depth + PLANES, 2 * modes_x), F32),
            left,
            left,
            weight,
            weight,
            right,
            right,
            pltpu.VMEM((2 * modes_y, 24), BF16),
            pltpu.VMEM((2 * modes_x, 24), BF16),
            pltpu.VMEM((2, 2 * depth, 8, modes_x), F32),
            pltpu.SemaphoreType.DMA,
            pltpu.SemaphoreType.DMA((2,)),
        ],
        name="spread",
    )(everyone, jnp.asarray(depth_table(depth)))
    return volume.reshape(2, depth, modes_y, modes_x)


def solution(mesh):
    placed = (
        P(("slab", "pencil"), None),
        P(None, ("slab", "pencil")),
        P(None, ("slab", "pencil")),
        P(None, ("slab", "pencil")),
    )
    return jax.shard_map(
        shards,
        mesh=mesh,
        in_specs=placed,
        out_specs=P(None, None, "slab", "pencil"),
        check_vma=False,
    )
```

time: 84.3 us -> 75.9 us (0.900)
  Pallas kernels: 64.1 us -> 57.6 us
  local copies, waits for them, and re-layouts: 2.19 us -> 0 us
    pallas_call x1, Pallas kernels: 62.2 us -> 55.9 us  [shards(): pl.pallas_call(lambda *refs: spread_kernel(n_slab, modes_y, modes_x, *ref...]
    unnamed x1 -> x0, local copies, waits for them, and re-layouts: 1.47 us -> none
where the time goes in v2:
time: 75.9 us; the launch traced here: 75.6 us
  Pallas kernels  57.6 us (76%)
  blocking collectives  18 us (24%)
    pallas_call x1, Pallas kernels, shards(): pl.pallas_call(lambda *refs: spread_kernel(n_slab, modes_y, modes_x, *ref...  55.9 us
    all_to_all x1, blocking collectives, shards(): lax.all_to_all(sent, ('slab', 'pencil'), split_axis=0, concat_axis=0, til...  18 us
    pallas_call x1, Pallas kernels, shards(): pl.pallas_call(lambda *refs: order_kernel(n_pencil, *refs), out_shape=jax...  1.77 us

profile of v2, /device:TPU:0, one launch (start us, length us, event | category | flops | bytes accessed | tf_op | source)
XLA Modules:
  0.0 75.6 jit_solution(15181780679962634938)
XLA Ops:
  0.0 1.8 %order.1 = f32[32,8,256]{2,1,0:T(8,128)} custom-call(s32[1,256]{1,0:T(1,128)} %bitcast.2, s32[3,256]{1,0:T(4,128)} %refs_1_.2, f32[3,256]{1,0:T(4,128)} %refs_2_.1, f32[2,256]{1,0:T(2,128)} %refs_3_.1), custom_call_target="tpu_custom_call" | custom-call | tf_op jit(solution)/shard_map/order/pallas_call | solution.py:372
  1.8 18.0 %all_to_all.5.refs_0_ = f32[32,8,256]{2,1,0:T(8,128)} all-to-all(f32[32,8,256]{2,1,0:T(8,128)} %order.1), channel_id=1, replica_groups=mesh['slab'=8,'pencil'=4] {'slab','pencil'}, dimensions={0} | all-to-all | bytes 524288 | tf_op jit(solution)/shard_map/all_to_all | solution.py:379
  19.8 55.9 %spread.1 = f32[128,64,128]{2,1,0:T(8,128)} custom-call(f32[32,8,256]{2,1,0:T(8,128)} %all_to_all.5.refs_0_, bf16[128,384]{1,0:T(8,128)(2,1)} %constant.2.clone.refs_1_), custom_call_target="tpu_custom_call" | custom-call | tf_op jit(solution)/shard_map/spread/pallas_call | solution.py:386
